TPU v7x, 32 devices: a whole 2x2x4 slice. The times are simulated.
32 devices in a mesh: seg: 4 (over y, x), lat: 8 (over z, core).
Axes of the slice: x: 2, y: 2, z: 4, core: 2. Of those that a mesh axis runs over, the one named last changes fastest.
Arguments:
- coh_map: bfloat16 [4, 65536, 128], P('seg', 'lat'), may hold values from 0 to 40, as said below
- positions: int32 [4, 1024], P('seg', 'lat'), may hold values from 0 to 16776959, as said below
- counts: int32 [16], P('lat'), may hold values from 1 to 64, as said below
Outputs:
- semi_stat: bfloat16 [1024, 128], P('lat')
- excess: float32 [16, 128], P('lat')
Inputs may be any that keep to these rules, and one draw needn't show every extreme that they name: `coh_map`: nonnegative. `counts`: the first block has 1 valid point and the last block 64. `positions`: the bins are split into 8 aligned slices of 8192 bins; a point's two bins lie in the same slice; in each segment, at most 32 of the 128 points of one index of lat have their bins in one slice, and that most is reached in every draw.
All inputs are finite; a program needn't handle non-finite values.
Results may differ from a plain program's by a relative error of at most 0.001.
Values sent between devices are 32-bit elements; how exact they have to be, the bound alone decides.
A program may use at most 64 MiB of HBM per device.

v0:
```python
import jax
import jax.numpy as jnp
from jax import lax
from jax.sharding import PartitionSpec as P


def routed_sums(positions, coh_map, first_bin):
    seg_count = coh_map.shape[0]
    slice_bins = coh_map.shape[1]
    width = coh_map.shape[2]
    own_rows = positions.shape[1]
    n_lataxis = lax.axis_size("lat")
    slot_limit = 2 * own_rows // n_lataxis
    dest = positions // 256 // slice_bins
    dest_hits = (dest[:, :, None] == lax.broadcasted_iota(jnp.int32, (1, 1, n_lataxis), 2)).astype(
        jnp.int32
    )
    before = jnp.cumsum(dest_hits, axis=1) - dest_hits
    slot = jnp.sum(before * dest_hits, axis=2)
    seg_ids = lax.broadcasted_iota(jnp.int32, positions.shape, 0)
    outgoing = (
        jnp.full((n_lataxis, seg_count, slot_limit), -1, jnp.int32)
        .at[dest, seg_ids, slot]
        .set(positions)
    )
    bin_index = lax.broadcasted_iota(jnp.int32, (1, slice_bins), 1)
    incoming = lax.all_to_all(outgoing, "lat", split_axis=0, concat_axis=0, tiled=True)
    item_count = incoming.shape[2]
    pos_flat = incoming[:, 0, :].reshape(-1)
    live = (pos_flat >= 0)[:, None]
    rel_bin = (pos_flat // 256 - first_bin)[:, None]
    fraction = (pos_flat % 256).astype(jnp.float32)[:, None] / 256.0
    weights = jnp.where(live & (bin_index == rel_bin), 1.0 - fraction, 0.0) + jnp.where(
        live & (bin_index == rel_bin + 1), fraction, 0.0
    )
    rows = jnp.dot(weights.astype(jnp.bfloat16), coh_map[0], preferred_element_type=jnp.float32)
    row_list = [rows.reshape(n_lataxis, item_count, width)]
    stacked = jnp.stack(row_list, axis=1)
    returned = lax.all_to_all(stacked, "lat", split_axis=0, concat_axis=0, tiled=True)
    by_segment = returned.transpose(1, 0, 2, 3).reshape(seg_count, n_lataxis * slot_limit, width)
    flat_index = dest * slot_limit + slot
    picked = jnp.take_along_axis(by_segment, flat_index[:, :, None], axis=1)
    return jnp.sum(picked, axis=0)


def shards(coh_map, positions, counts):
    seg_count = coh_map.shape[0]
    slice_bins = coh_map.shape[1]
    first_bin = lax.axis_index("lat") * slice_bins
    n_segaxis = lax.axis_size("seg")
    total_segs = seg_count * n_segaxis
    own_rows = positions.shape[1]
    local_sums_rows = routed_sums(positions, coh_map, first_bin)
    summed = lax.psum(local_sums_rows, "seg")
    semi_stat = summed / total_segs
    block_count = counts.shape[0]
    block_size = own_rows // block_count
    grouped = semi_stat.reshape(block_count, block_size, semi_stat.shape[1])
    slot_index = lax.broadcasted_iota(jnp.int32, (block_count, block_size, 1), 1)
    live_mask = slot_index < counts[:, None, None]
    block_sums = jnp.sum(jnp.where(live_mask, grouped, 0.0), axis=1)
    count_float = counts.astype(jnp.float32)
    block_means = block_sums / count_float[:, None]
    column_sums, total_count = lax.psum((jnp.sum(block_sums, axis=0), jnp.sum(count_float)), "lat")
    global_mean = column_sums / total_count
    excess = block_means - global_mean[None, :]
    return (semi_stat.astype(jnp.bfloat16), excess)


def solution(mesh):
    in_specs = (P("seg", "lat", None), P("seg", "lat"), P("lat"))
    out_specs = (P("lat", None), P("lat", None))
    return jax.shard_map(shards, mesh=mesh, in_specs=in_specs, out_specs=out_specs, check_vma=False)
```

profile of v0, /device:TPU:0, one launch (start us, length us, event | category | flops | bytes accessed | tf_op | source)
XLA Modules:
  0.0 125.4 jit_solution(7126655053401794815)
XLA Ops:
  7.2 0.0 copy-start
  7.2 0.8 fusion.19
  8.0 0.1 fusion.12
  8.1 0.2 reduce_window_sum.11
  8.3 0.2 select_reduce_fusion.2
  8.5 0.6 broadcast.427
  9.1 19.9 %scatter_fusion = s32[8,32]{1,0:T(8,128)} fusion(s32[8,32]{1,0:T(8,128)} %broadcast.427, s32[128]{0:T(128)S(1)} %fusion.21, s32[128]{0:T(128)} %bitcast.50), kind=kCustom, calls=%fused_computation.1 | custom fusion | bytes 2560 | tf_op jit(solution)/shard_map/scatter | solution.py:24
  29.0 6.4 %all-to-all-start = ((s32[8,1,32]{2,1,0:T(1,128)}), s32[8,1,32]{2,1,0:T(1,128)S(1)}, u32[]{:S(2)}, u32[]{:S(2)}) async-start(s32[8,1,32]{2,1,0:T(1,128)} %bitcast.9), calls=%async_computation | async-start | bytes 8192 | tf_op jit(solution)/shard_map/all_to_all | solution.py:27
  35.3 0.7 iota_compare_fusion.3
  36.0 4.8 %all-to-all-done = s32[8,1,32]{2,1,0:T(1,128)S(1)} async-done(((s32[8,1,32]{2,1,0:T(1,128)}), s32[8,1,32]{2,1,0:T(1,128)S(1)}, u32[]{:S(2)}, u32[]{:S(2)}) %all-to-all-start) | async-done | bytes 1056 | tf_op jit(solution)/shard_map/all_to_all | solution.py:27
  40.9 0.0 copy-done
  40.9 0.0 copy-start.1
  40.9 5.0 %fusion.7 = f32[8,1,32,128]{3,2,1,0:T(8,128)} fusion(bf16[1,8192,128]{2,1,0:T(8,128)(2,1)S(1)} %copy-done, f32[8,32]{1,0:T(8,128)S(1)} %get-tuple-element.5, s32[8,32]{1,0:T(8,128)S(1)} %get-tuple-element.6, f32[8,32]{1,0:T(8,128)S(1)} %get-tuple-element.4, s32[8,32]{1,0:T(8,128)S(1)} %get-tuple-element.7, pred[8,32]{1,0:T(8,128)(4,1)S(1)} %broadcast_compare_fusion), kind=kOutput, calls=%fused_computation.11 | convolution fusion | flops 553648128 | bytes 2232576 | tf_op jit(solution)/shard_map/dot_general | solution.py:36
  45.9 3.4 %all-to-all-start.1 = ((f32[8,1,32,128]{3,2,1,0:T(8,128)}), f32[8,1,32,128]{3,2,1,0:T(8,128)S(1)}, u32[]{:S(2)}, u32[]{:S(2)}) async-start(f32[8,1,32,128]{3,2,1,0:T(8,128)} %fusion.7), calls=%async_computation.1 | async-start | bytes 262144 | tf_op jit(solution)/shard_map/all_to_all | solution.py:39
  49.2 0.0 all-reduce.3.cloned.1.call-start
  49.3 0.0 copy-done.1
  49.3 0.1 lt.77
  49.4 6.5 %all-to-all-done.1 = f32[8,1,32,128]{3,2,1,0:T(8,128)S(1)} async-done(((f32[8,1,32,128]{3,2,1,0:T(8,128)}), f32[8,1,32,128]{3,2,1,0:T(8,128)S(1)}, u32[]{:S(2)}, u32[]{:S(2)}) %all-to-all-start.1) | async-done | bytes 131104 | tf_op jit(solution)/shard_map/all_to_all | solution.py:39
  55.9 0.6 gather_fusion
  56.6 0.7 broadcast_select_fusion
  57.3 0.0 all-reduce.3.cloned.1.call-update
  57.3 0.6 convert_reduce_fusion
  57.9 40.4 %all-reduce.3.cloned.1.call-done = f32[128,128]{1,0:T(8,128)} async-done(((f32[128,128]{1,0:T(8,128)}), f32[128,128]{1,0:T(8,128)}) %all-reduce.3.cloned.1.call-update) | async-done | bytes 65552 | tf_op jit(solution)/shard_map/psum | solution.py:54
  98.3 1.5 %select_reduce_fusion = (f32[128]{0:T(128)S(1)}, bf16[128,128]{1,0:T(8,128)(2,1)}) fusion(pred[128]{0:T(512)(128)(4,1)S(1)} %lt.77, f32[128,128]{1,0:T(8,128)} %all-reduce.3.cloned.1.call-done), kind=kLoop, calls=%fused_computation.12 | loop fusion | flops 65408 | bytes 98944 | tf_op jit(solution)/shard_map/reduce_sum | solution.py:64
  99.8 16.6 %all-reduce = (f32[128]{0:T(128)S(1)}, f32[]{:T(128)}) all-reduce(f32[128]{0:T(128)S(1)} %get-tuple-element.10, f32[]{:T(128)} %convert_reduce_fusion), channel_id=1, replica_groups=mesh['seg'=4,'lat'=8] {'lat'}, use_global_device_ids=true, to_apply=%region_6.7 | all-reduce | flops 129 | bytes 1032 | tf_op jit(solution)/shard_map/psum | solution.py:64
  116.3 0.6 broadcast_divide_fusion
  117.0 0.9 select_reduce_fusion.1
  117.9 0.6 divide_subtract_fusion
  (11 shorter events, 0.1 us)
Async XLA Ops:
  7.2 33.7 %copy-start = (bf16[1,8192,128]{2,1,0:T(8,128)(2,1)S(1)}, bf16[1,8192,128]{2,1,0:T(8,128)(2,1)}, u32[]{:S(2)}) copy-start(bf16[1,8192,128]{2,1,0:T(8,128)(2,1)} %param.3) | copy-start | bytes 6291460
  29.0 11.9 %all-to-all-start = ((s32[8,1,32]{2,1,0:T(1,128)}), s32[8,1,32]{2,1,0:T(1,128)S(1)}, u32[]{:S(2)}, u32[]{:S(2)}) async-start(s32[8,1,32]{2,1,0:T(1,128)} %bitcast.9), calls=%async_computation | async-start | bytes 8192 | tf_op jit(solution)/shard_map/all_to_all | solution.py:27
  40.9 8.4 %copy-start.1 = (s32[2]{0:T(128)S(1)}, s32[2]{0:T(128)}, u32[]{:S(2)}) copy-start(s32[2]{0:T(128)} %param.5) | copy-start | bytes 28
  45.9 10.1 %all-to-all-start.1 = ((f32[8,1,32,128]{3,2,1,0:T(8,128)}), f32[8,1,32,128]{3,2,1,0:T(8,128)S(1)}, u32[]{:S(2)}, u32[]{:S(2)}) async-start(f32[8,1,32,128]{3,2,1,0:T(8,128)} %fusion.7), calls=%async_computation.1 | async-start | bytes 262144 | tf_op jit(solution)/shard_map/all_to_all | solution.py:39
  49.2 49.1 %all-reduce.3.cloned.1.call-start = ((), (), s32[]{:S(2)}) async-start(), calls=%async_computation.2 | async-start | bytes 131072 | tf_op jit(solution)/shard_map/psum | solution.py:54
Sparse Core Ops, SparseCore 0:
  57.4 40.8 all-reduce.2
where the time goes:
time: 126 us; the launch traced here: 125 us
  waiting for transfers between devices  51.7 us (41%)
  local copies, waits for them, and re-layouts  21.2 us (17%)
  blocking collectives  16.6 us (13%)
  between operations  14.1 us (11%)
  starting transfers between devices  9.76 us (8%)
  other arithmetic  7.05 us (6%)
  matrix products  4.96 us (4%)
    psum x1, waiting for transfers between devices, shards(): summed = lax.psum(local_sums_rows, 'seg')  40.4 us
    scatter x1, local copies, waits for them, and re-layouts, routed_sums(): outgoing = jnp.full((n_lataxis, seg_count, slot_limit), -1, jnp.int32).at...  19.9 us
    psum x1, blocking collectives, shards(): lax.psum((jnp.sum(block_sums, axis=0), jnp.sum(count_float)), 'lat')  16.6 us
    all_to_all x1, waiting for transfers between devices, routed_sums(): lax.all_to_all(stacked, 'lat', split_axis=0, concat_axis=0, tiled=True)  6.51 us
    all_to_all x1, starting transfers between devices, routed_sums(): lax.all_to_all(outgoing, 'lat', split_axis=0, concat_axis=0, tiled=True)  6.35 us
    dot_general x1, matrix products, routed_sums(): jnp.dot(weights.astype(jnp.bfloat16), coh_map[0], preferred_element_type=...  4.96 us
    all_to_all x1, waiting for transfers between devices, routed_sums(): lax.all_to_all(outgoing, 'lat', split_axis=0, concat_axis=0, tiled=True)  4.77 us
    all_to_all x1, starting transfers between devices, routed_sums(): lax.all_to_all(stacked, 'lat', split_axis=0, concat_axis=0, tiled=True)  3.37 us
  transfers between devices with their start and end apart: 3, of which 3 were waited for; matrix products, arithmetic and copies ran while one was open for 1% of the time, Pallas kernels for 0%

commit v1 on v0

--- a/solution.py
+++ b/solution.py
@@ -51,7 +51,9 @@
     total_segs = seg_count * n_segaxis
     own_rows = positions.shape[1]
     local_sums_rows = routed_sums(positions, coh_map, first_bin)
-    summed = lax.psum(local_sums_rows, "seg")
+    summed = local_sums_rows
+    for hop in (1, 2):
+        summed = summed + lax.ppermute(summed, "seg", [(dev, dev ^ hop) for dev in range(4)])
     semi_stat = summed / total_segs
     block_count = counts.shape[0]
     block_size = own_rows // block_count

time: 126 us -> 75.9 us (0.60)
  waiting for transfers between devices: 51.7 us -> 16.9 us
  between operations: 14.1 us -> 0.77 us
  starting transfers between devices: 9.76 us -> 12.9 us
  other arithmetic: 7.05 us -> 4.19 us
  blocking collectives: 16.6 us -> 14.2 us
    psum x1 -> x0, waiting for transfers between devices: 40.4 us -> none  [shards(): summed = lax.psum(local_sums_rows, 'seg')]
    ppermute x0 -> x2, waiting for transfers between devices: none -> 4.76 us  [shards(): lax.ppermute(summed, 'seg', [(dev, dev ^ hop) for dev in range(4)])]
    ppermute x0 -> x2, starting transfers between devices: none -> 3.14 us  [shards(): lax.ppermute(summed, 'seg', [(dev, dev ^ hop) for dev in range(4)])]
    psum x1, blocking collectives: 16.6 us -> 14.2 us  [shards(): lax.psum((jnp.sum(block_sums, axis=0), jnp.sum(count_float)), 'lat')]
  transfers between devices with their start and end apart: 3 -> 4, of which waited for: 3 -> 4; matrix products, arithmetic and copies ran while one was open for 1% -> 1% of each run, Pallas kernels for 0% -> 0%
where the time goes in v1:
time: 75.9 us; the launch traced here: 75.1 us
  local copies, waits for them, and re-layouts  21.2 us (28%)
  waiting for transfers between devices  16.9 us (22%)
  blocking collectives  14.2 us (19%)
  starting transfers between devices  12.9 us (17%)
  matrix products  4.96 us (7%)
  other arithmetic  4.19 us (6%)
  between operations  0.77 us (1%)
    scatter x1, local copies, waits for them, and re-layouts, routed_sums(): outgoing = jnp.full((n_lataxis, seg_count, slot_limit), -1, jnp.int32).at...  19.9 us
    psum x1, blocking collectives, shards(): lax.psum((jnp.sum(block_sums, axis=0), jnp.sum(count_float)), 'lat')  14.2 us
    all_to_all x1, waiting for transfers between devices, routed_sums(): lax.all_to_all(stacked, 'lat', split_axis=0, concat_axis=0, tiled=True)  6.66 us
    all_to_all x1, starting transfers between devices, routed_sums(): lax.all_to_all(outgoing, 'lat', split_axis=0, concat_axis=0, tiled=True)  6.35 us
    all_to_all x1, waiting for transfers between devices, routed_sums(): lax.all_to_all(outgoing, 'lat', split_axis=0, concat_axis=0, tiled=True)  5.5 us
    dot_general x1, matrix products, routed_sums(): jnp.dot(weights.astype(jnp.bfloat16), coh_map[0], preferred_element_type=...  4.96 us
    ppermute x2, waiting for transfers between devices, shards(): lax.ppermute(summed, 'seg', [(dev, dev ^ hop) for dev in range(4)])  4.76 us
    all_to_all x1, starting transfers between devices, routed_sums(): lax.all_to_all(stacked, 'lat', split_axis=0, concat_axis=0, tiled=True)  3.37 us
  transfers between devices with their start and end apart: 4, of which 4 were waited for; matrix products, arithmetic and copies ran while one was open for 1% of the time, Pallas kernels for 0%

profile of v1, /device:TPU:0, one launch (start us, length us, event | category | flops | bytes accessed | tf_op | source)
XLA Modules:
  0.0 75.1 jit_solution(16792370357827158864)
XLA Ops:
  0.6 0.0 copy-start
  0.6 0.8 %fusion.19 = (s32[1,128,1]{1,2,0:T(1,128)S(1)}, s32[1,128]{1,0:T(1,128)S(1)}) fusion(s32[1,128]{1,0:T(1,128)} %param.4), kind=kLoop, calls=%fused_computation.56 | loop fusion | flops 4224 | bytes 1536 | tf_op jit(solution)/shard_map/broadcast_in_dim | solution.py:24
  1.5 0.1 fusion.12
  1.6 0.2 reduce_window_sum.11
  1.7 0.2 select_reduce_fusion.2
  2.0 0.6 broadcast.427
  2.6 19.9 %scatter_fusion = s32[8,32]{1,0:T(8,128)} fusion(s32[8,32]{1,0:T(8,128)} %broadcast.427, s32[128]{0:T(128)S(1)} %fusion.21, s32[128]{0:T(128)} %bitcast.50), kind=kCustom, calls=%fused_computation.1 | custom fusion | bytes 2560 | tf_op jit(solution)/shard_map/scatter | solution.py:24
  22.4 6.4 %all-to-all-start = ((s32[8,1,32]{2,1,0:T(1,128)}), s32[8,1,32]{2,1,0:T(1,128)S(1)}, u32[]{:S(2)}, u32[]{:S(2)}) async-start(s32[8,1,32]{2,1,0:T(1,128)} %bitcast.9), calls=%async_computation | async-start | bytes 8192 | tf_op jit(solution)/shard_map/all_to_all | solution.py:27
  28.8 5.5 %all-to-all-done = s32[8,1,32]{2,1,0:T(1,128)S(1)} async-done(((s32[8,1,32]{2,1,0:T(1,128)}), s32[8,1,32]{2,1,0:T(1,128)S(1)}, u32[]{:S(2)}, u32[]{:S(2)}) %all-to-all-start) | async-done | bytes 1056 | tf_op jit(solution)/shard_map/all_to_all | solution.py:27
  34.3 0.0 copy-done
  34.3 0.0 copy-start.1
  34.4 5.0 %fusion.7 = f32[8,1,32,128]{3,2,1,0:T(8,128)} fusion(bf16[1,8192,128]{2,1,0:T(8,128)(2,1)S(1)} %copy-done, f32[8,32]{1,0:T(8,128)S(1)} %get-tuple-element.5, s32[8,32]{1,0:T(8,128)S(1)} %get-tuple-element.6, f32[8,32]{1,0:T(8,128)S(1)} %get-tuple-element.4, s32[8,32]{1,0:T(8,128)S(1)} %get-tuple-element.7, pred[8,32]{1,0:T(8,128)(4,1)S(1)} %broadcast_compare_fusion), kind=kOutput, calls=%fused_computation.11 | convolution fusion | flops 553648128 | bytes 2232576 | tf_op jit(solution)/shard_map/dot_general | solution.py:36
  39.3 3.4 %all-to-all-start.1 = ((f32[8,1,32,128]{3,2,1,0:T(8,128)}), f32[8,1,32,128]{3,2,1,0:T(8,128)S(1)}, u32[]{:S(2)}, u32[]{:S(2)}) async-start(f32[8,1,32,128]{3,2,1,0:T(8,128)} %fusion.7), calls=%async_computation.1 | async-start | bytes 262144 | tf_op jit(solution)/shard_map/all_to_all | solution.py:39
  42.7 6.7 %all-to-all-done.1 = f32[8,1,32,128]{3,2,1,0:T(8,128)S(1)} async-done(((f32[8,1,32,128]{3,2,1,0:T(8,128)}), f32[8,1,32,128]{3,2,1,0:T(8,128)S(1)}, u32[]{:S(2)}, u32[]{:S(2)}) %all-to-all-start.1) | async-done | bytes 131104 | tf_op jit(solution)/shard_map/all_to_all | solution.py:39
  49.4 0.6 gather_fusion
  50.0 0.1 broadcast_select_fusion
  50.1 1.6 %collective-permute-start = (f32[128,128]{1,0:T(8,128)S(1)}, f32[128,128]{1,0:T(8,128)S(1)}, u32[]{:S(2)}, u32[]{:S(2)}) collective-permute-start(f32[128,128]{1,0:T(8,128)S(1)} %broadcast_select_fusion), channel_id=1, source_target_pairs={{0,8},{8,0},{16,24},{24,16},{1,9},{9,1},{17,25},{25,17},{2,10},{10... | collective-permute-start | bytes 196616 | tf_op jit(solution)/shard_map/ppermute | solution.py:56
  51.7 0.0 copy-done.1
  51.7 0.1 iota_compare_fusion.3
  51.8 0.1 lt.77
  51.8 2.6 %collective-permute-done = f32[128,128]{1,0:T(8,128)S(1)} collective-permute-done((f32[128,128]{1,0:T(8,128)S(1)}, f32[128,128]{1,0:T(8,128)S(1)}, u32[]{:S(2)}, u32[]{:S(2)}) %collective-permute-start) | collective-permute-done | bytes 65568 | tf_op jit(solution)/shard_map/ppermute | solution.py:56
  54.4 0.1 fusion.26
  54.5 1.6 %collective-permute-start.1 = (f32[128,128]{1,0:T(8,128)S(1)}, f32[128,128]{1,0:T(8,128)S(1)}, u32[]{:S(2)}, u32[]{:S(2)}) collective-permute-start(f32[128,128]{1,0:T(8,128)S(1)} %fusion.26), channel_id=1, source_target_pairs={{0,16},{8,24},{16,0},{24,8},{1,17},{9,25},{17,1},{25,9},{2,18},{10... | collective-permute-start | bytes 196616 | tf_op jit(solution)/shard_map/ppermute | solution.py:56
  56.1 0.6 convert_reduce_fusion
  56.7 2.1 %collective-permute-done.1 = f32[128,128]{1,0:T(8,128)S(1)} collective-permute-done((f32[128,128]{1,0:T(8,128)S(1)}, f32[128,128]{1,0:T(8,128)S(1)}, u32[]{:S(2)}, u32[]{:S(2)}) %collective-permute-start.1) | collective-permute-done | bytes 65568 | tf_op jit(solution)/shard_map/ppermute | solution.py:56
  58.9 0.6 select_reduce_fusion
  59.5 14.2 %all-reduce = (f32[128]{0:T(128)S(1)}, f32[]{:T(128)}) all-reduce(f32[128]{0:T(128)S(1)} %get-tuple-element.10, f32[]{:T(128)} %convert_reduce_fusion), channel_id=1, replica_groups=mesh['seg'=4,'lat'=8] {'lat'}, use_global_device_ids=true, to_apply=%region_5.6 | all-reduce | flops 129 | bytes 1032 | tf_op jit(solution)/shard_map/psum | solution.py:66
  73.7 0.6 broadcast_divide_fusion
  74.4 0.1 select_reduce_fusion.1
  74.5 0.6 divide_subtract_fusion
  (11 shorter events, 0.1 us)
Async XLA Ops:
  0.6 33.7 %copy-start = (bf16[1,8192,128]{2,1,0:T(8,128)(2,1)S(1)}, bf16[1,8192,128]{2,1,0:T(8,128)(2,1)}, u32[]{:S(2)}) copy-start(bf16[1,8192,128]{2,1,0:T(8,128)(2,1)} %param.3) | copy-start | bytes 6291460
  22.4 11.9 %all-to-all-start = ((s32[8,1,32]{2,1,0:T(1,128)}), s32[8,1,32]{2,1,0:T(1,128)S(1)}, u32[]{:S(2)}, u32[]{:S(2)}) async-start(s32[8,1,32]{2,1,0:T(1,128)} %bitcast.9), calls=%async_computation | async-start | bytes 8192 | tf_op jit(solution)/shard_map/all_to_all | solution.py:27
  34.3 17.3 %copy-start.1 = (s32[2]{0:T(128)S(1)}, s32[2]{0:T(128)}, u32[]{:S(2)}) copy-start(s32[2]{0:T(128)} %param.5) | copy-start | bytes 28
  39.3 10.1 %all-to-all-start.1 = ((f32[8,1,32,128]{3,2,1,0:T(8,128)}), f32[8,1,32,128]{3,2,1,0:T(8,128)S(1)}, u32[]{:S(2)}, u32[]{:S(2)}) async-start(f32[8,1,32,128]{3,2,1,0:T(8,128)} %fusion.7), calls=%async_computation.1 | async-start | bytes 262144 | tf_op jit(solution)/shard_map/all_to_all | solution.py:39
  50.1 4.3 %collective-permute-start = (f32[128,128]{1,0:T(8,128)S(1)}, f32[128,128]{1,0:T(8,128)S(1)}, u32[]{:S(2)}, u32[]{:S(2)}) collective-permute-start(f32[128,128]{1,0:T(8,128)S(1)} %broadcast_select_fusion), channel_id=1, source_target_pairs={{0,8},{8,0},{16,24},{24,16},{1,9},{9,1},{17,25},{25,17},{2,10},{10... | collective-permute-start | bytes 196616 | tf_op jit(solution)/shard_map/ppermute | solution.py:56
  54.5 4.3 %collective-permute-start.1 = (f32[128,128]{1,0:T(8,128)S(1)}, f32[128,128]{1,0:T(8,128)S(1)}, u32[]{:S(2)}, u32[]{:S(2)}) collective-permute-start(f32[128,128]{1,0:T(8,128)S(1)} %fusion.26), channel_id=1, source_target_pairs={{0,16},{8,24},{16,0},{24,8},{1,17},{9,25},{17,1},{25,9},{2,18},{10... | collective-permute-start | bytes 196616 | tf_op jit(solution)/shard_map/ppermute | solution.py:56
